TPU v7x, 32 devices: a whole 2x2x4 slice. The times are simulated.
32 devices in a mesh: seq: 8 (over z, x), head: 4 (over y, core).
Axes of the slice: x: 2, y: 2, z: 4, core: 2. Of those that a mesh axis runs over, the one named last changes fastest.
Arguments:
- x_in: bfloat16 [4096, 5120], P('seq', 'head'), may hold values from -9 to 9
- z_gate: bfloat16 [4096, 5120], P('seq', 'head'), may hold values from -6 to 6
- bc_in: bfloat16 [4096, 256], P('seq'), may hold values from -6 to 6
- conv_x: float32 [4, 5120], P(None, 'head'), may hold values from -3 to 3
- conv_bc: float32 [4, 256], replicated, may hold values from -3 to 3
- dt_raw: float32 [80, 4096], P('head', 'seq'), may hold values from -3 to 3
- dt_bias: float32 [80], P('head'), may hold values from -3.3 to 0.3
- a_log: float32 [80], P('head'), may hold values from -25 to -1
- skip_d: float32 [80], P('head'), may hold values from 0.5 to 1.5
- norm_weight: float32 [5120], replicated, may hold values from 0.5 to 1.5
- w_out: bfloat16 [5120, 2560], P('head'), may hold values from -0.078125 to 0.078125
Outputs:
- mixed_out: bfloat16 [4096, 2560], P(('seq', 'head'))
All inputs are finite; a program needn't handle non-finite values.
Results may differ from a plain program's by a relative error of at most 0.014.
Values may be sent and summed in bfloat16 or wider, within the bound.
A program may use at most 128 MiB of HBM per device.

v0:
```python
import jax
import jax.numpy as jnp
from jax import lax
from jax.sharding import PartitionSpec as P

HEAD_DIM = 64
STATE = 128
CONV = 4
GROUP = 128
D_INNER = 5120


epsilon = 1e-05


def passed_along(block, axis, distance):
    devices = range(lax.axis_size(axis))
    route = [(i - distance, i) for i in devices if i - distance in devices]
    return lax.ppermute(block, axis, route)


def conv_silu(extended, kernel, length):
    summed = kernel[0] * extended[0:length].astype(jnp.float32)
    for k in range(1, kernel.shape[0]):
        summed = summed + kernel[k] * extended[k : k + length].astype(jnp.float32)
    return jax.nn.silu(summed).astype(jnp.bfloat16)


def combine(former, latter):
    return (former[0] * latter[0], latter[0][:, None, None] * former[1] + latter[1])


def per_device(
    x_in, z_gate, bc_in, conv_x, conv_bc, dt_raw, dt_bias, a_log, skip_d, norm_weight, w_out
):
    tok_rows = x_in.shape[0]
    head_count = dt_raw.shape[0]
    nblock = tok_rows // GROUP
    rim_width = CONV - 1
    prev_x, prev_bc = passed_along(
        (x_in[tok_rows - rim_width :], bc_in[tok_rows - rim_width :]), "seq", 1
    )
    x_conv = conv_silu(jnp.concatenate([prev_x, x_in], axis=0), conv_x, tok_rows)
    bc_conv = conv_silu(jnp.concatenate([prev_bc, bc_in], axis=0), conv_bc, tok_rows)
    step_size = jax.nn.softplus(dt_raw + dt_bias[:, None])
    log_decay = step_size * (-jnp.exp(a_log))[:, None]
    x_blocks = x_conv.reshape(nblock, GROUP, head_count, HEAD_DIM)
    b_blocks = bc_conv[:, :STATE].reshape(nblock, GROUP, STATE)
    c_blocks = bc_conv[:, STATE:].reshape(nblock, GROUP, STATE)
    d_blocks = step_size.reshape(head_count, nblock, GROUP).transpose(1, 0, 2)
    cumulative = jnp.cumsum(log_decay.reshape(head_count, nblock, GROUP).transpose(1, 0, 2), axis=2)
    group_ends = cumulative[:, :, -1]
    to_end = jnp.exp(group_ends[:, :, None] - cumulative) * d_blocks
    scaled = (x_blocks * jnp.transpose(to_end, (0, 2, 1))[:, :, :, None]).astype(jnp.bfloat16)
    local_terms = jnp.einsum("cshp,csn->chpn", scaled, b_blocks, preferred_element_type=jnp.float32)
    causal = jnp.arange(GROUP)[:, None] >= jnp.arange(GROUP)[None, :]
    c_dot_b = jnp.einsum("ctn,csn->cts", c_blocks, b_blocks, preferred_element_type=jnp.float32)
    segment = cumulative[:, :, :, None] - cumulative[:, :, None, :]
    decays = jnp.where(causal, jnp.exp(jnp.where(causal, segment, 0.0)), 0.0)
    mixer = (c_dot_b[:, None] * decays * d_blocks[:, :, None, :]).astype(jnp.bfloat16)
    y_diag = jnp.einsum("chts,cshp->cthp", mixer, x_blocks, preferred_element_type=jnp.float32)
    running = jnp.zeros((head_count, HEAD_DIM, STATE), jnp.float32)
    carried = jnp.ones((head_count,), jnp.float32)
    local_entering = []
    decay_before = []
    for c in range(nblock):
        local_entering.append(running)
        decay_before.append(carried)
        block_decay = jnp.exp(group_ends[c])
        running = block_decay[:, None, None] * running + local_terms[c]
        carried = carried * block_decay
    position = lax.axis_index("seq")
    summary = (carried, running)
    for k in range((lax.axis_size("seq") - 1).bit_length()):
        reach = 2**k
        former = passed_along((summary[0], summary[1]), "seq", reach)
        merged = combine(former, summary)
        taken = position >= reach
        summary = (jnp.where(taken, merged[0], summary[0]), jnp.where(taken, merged[1], summary[1]))
    incoming = passed_along(summary[1].astype(jnp.bfloat16), "seq", 1).astype(jnp.float32)
    entering = jnp.stack(
        [
            (local_entering[c] + decay_before[c][:, None, None] * incoming).astype(jnp.bfloat16)
            for c in range(nblock)
        ]
    )
    y_off = jnp.einsum("ctn,chpn->cthp", c_blocks, entering, preferred_element_type=jnp.float32)
    y_off = y_off * jnp.exp(jnp.transpose(cumulative, (0, 2, 1)))[:, :, :, None]
    output = y_diag + y_off + skip_d[None, None, :, None] * x_blocks
    output = output.reshape(tok_rows, head_count * HEAD_DIM)
    gated = (output * jax.nn.silu(z_gate.astype(jnp.float32))).astype(jnp.bfloat16)
    gated_f = gated.astype(jnp.float32)
    partial_sums = jnp.sum(gated_f * gated_f, axis=1)
    sum_squares = lax.psum(partial_sums, "head")
    inv_rms = lax.rsqrt(sum_squares / D_INNER + epsilon)
    local_cols = gated.shape[1]
    local_gain = lax.dynamic_slice_in_dim(
        norm_weight, lax.axis_index("head") * local_cols, local_cols
    )
    normed = (gated_f * inv_rms[:, None] * local_gain[None, :]).astype(jnp.bfloat16)
    return lax.psum_scatter(
        jnp.dot(normed, w_out, preferred_element_type=jnp.float32).astype(jnp.bfloat16),
        "head",
        scatter_dimension=0,
        tiled=True,
    )


def solution(mesh):
    in_specs = (
        P("seq", "head"),
        P("seq", "head"),
        P("seq", None),
        P(None, "head"),
        P(),
        P("head", "seq"),
        P("head"),
        P("head"),
        P("head"),
        P(),
        P("head", None),
    )
    out_specs = P(("seq", "head"), None)
    return jax.shard_map(
        per_device, mesh=mesh, in_specs=in_specs, out_specs=out_specs, check_vma=False
    )
```

profile of v0, /device:TPU:25, one launch (start us, length us, event | category | flops | bytes accessed | tf_op | source)
XLA Modules:
  0.0 172.3 jit_solution(16913806438401887070)
XLA Ops:
  6.5 0.8 slice.90
  7.3 0.3 copy.13
  7.6 3.1 %collective-permute-start = (bf16[3,1280]{0,1:T(8,128)(2,1)S(1)}, bf16[3,1280]{0,1:T(8,128)(2,1)S(1)}, u32[]{:S(2)}, u32[]{:S(2)}) collective-permute-start(bf16[3,1280]{0,1:T(8,128)(2,1)S(1)} %copy.13), channel_id=1, source_target_pairs={{0,4},{4,8},{8,12},{12,16},{16,20},{20,24},{24,28},{1,5},{5,9},{9,... | collective-permute-start | bytes 23048 | tf_op jit(solution)/shard_map/ppermute | solution.py:19
  10.7 0.7 slice.98
  11.4 1.9 %collective-permute-start.1 = (bf16[3,256]{1,0:T(4,128)(2,1)S(1)}, bf16[3,256]{1,0:T(4,128)(2,1)S(1)}, u32[]{:S(2)}, u32[]{:S(2)}) collective-permute-start(bf16[3,256]{1,0:T(4,128)(2,1)S(1)} %slice.98), channel_id=1, source_target_pairs={{0,4},{4,8},{8,12},{12,16},{16,20},{20,24},{24,28},{1,5},{5,9},{9,... | collective-permute-start | bytes 4616 | tf_op jit(solution)/shard_map/ppermute | solution.py:19
  13.3 0.7 exponential_negate_fusion
  14.0 0.9 broadcast_multiply_fusion
  14.9 1.2 reduce_window_sum.11
  16.1 0.2 slice_reduce_fusion
  16.3 0.2 fusion.51
  16.6 0.8 fusion.60
  17.4 0.1 bitcast_multiply_fusion
  17.5 0.6 fusion.57
  18.1 1.5 slice_reduce_fusion.4
  19.6 1.6 copy.14
  21.3 0.3 multiply_convert_fusion.3
  21.6 0.7 fusion.59
  22.3 3.7 %multiply_convert_fusion.2 = bf16[512,1280]{0,1:T(8,128)(2,1)S(1)} fusion(bf16[512,1280]{0,1:T(8,128)(2,1)S(1)} %copy.14, bf16[3,1280]{0,1:T(8,128)(2,1)S(1)} %collective-permute-done, f32[1280]{0:T(1024)} %get-tuple-element.11, f32[1280]{0:T(1024)} %get-tuple-element.12, f32[1280]{0:T(1024)} %get-tuple-element.10, f32[1280]{0:T(1024)S(1)} %get-tuple-element.9), kind=kLoop, calls=%fused_computation.24 | loop fusion | flops 16384000 | bytes 2649600 | tf_op jit(solution)/shard_map/convert_element_type | solution.py:26
  26.1 1.2 reshape.93
  27.3 1.8 %fusion.20 = f32[4,20,64,128]{3,2,1,0:T(8,128)S(1)} fusion(bf16[4,128,128,1]{2,1,3,0:T(8,128)(2,1)S(1)} %bitcast.80, f32[4,128,20]{1,2,0:T(8,128)S(1)} %bitcast_multiply_fusion, bf16[4,128,20,64]{1,0,3,2:T(4,128)(2,1)} %reshape.93), kind=kOutput, calls=%fused_computation.33 | convolution fusion | flops 169738240 | bytes 4104192 | tf_op jit(solution)/shard_map/cshp,csn->chpn/dot_general | solution.py:55
  29.2 1.1 fusion.41
  30.3 1.9 %collective-permute-start.4 = (f32[20,64,128]{2,1,0:T(8,128)S(1)}, f32[20,64,128]{2,1,0:T(8,128)}, u32[]{:S(2)}, u32[]{:S(2)}) collective-permute-start(f32[20,64,128]{2,1,0:T(8,128)S(1)} %get-tuple-element.18), channel_id=1, source_target_pairs={{0,4},{4,8},{8,12},{12,16},{16,20},{20,24},{24,28},{1,5},{5,9},{9,... | collective-permute-start | bytes 1966088 | tf_op jit(solution)/shard_map/ppermute | solution.py:19
  32.2 16.3 %collective-permute-done.4 = f32[20,64,128]{2,1,0:T(8,128)} collective-permute-done((f32[20,64,128]{2,1,0:T(8,128)S(1)}, f32[20,64,128]{2,1,0:T(8,128)}, u32[]{:S(2)}, u32[]{:S(2)}) %collective-permute-start.4) | collective-permute-done | bytes 655392 | tf_op jit(solution)/shard_map/ppermute | solution.py:19
  48.5 1.4 add_select_fusion.2
  49.9 1.3 collective-permute-start.5
  51.2 1.9 %collective-permute-start.2 = (f32[20]{0:T(128)}, f32[20]{0:T(128)}, u32[]{:S(2)}, u32[]{:S(2)}) collective-permute-start(f32[20]{0:T(128)} %get-tuple-element.15), channel_id=1, source_target_pairs={{0,4},{4,8},{8,12},{12,16},{16,20},{20,24},{24,28},{1,5},{5,9},{9,... | collective-permute-start | bytes 248 | tf_op jit(solution)/shard_map/ppermute | solution.py:19
  53.2 2.4 %copy.22 = bf16[512,1280]{0,1:T(8,128)(2,1)} copy(bf16[512,1280]{1,0:T(8,128)(2,1)} %param.12) | data formatting | bytes 2621440 | tf_op args[1]
  55.7 10.0 %collective-permute-done.2 = f32[20]{0:T(128)} collective-permute-done((f32[20]{0:T(128)}, f32[20]{0:T(128)}, u32[]{:S(2)}, u32[]{:S(2)}) %collective-permute-start.2) | collective-permute-done | bytes 112 | tf_op jit(solution)/shard_map/ppermute | solution.py:19
  65.7 0.7 broadcast_select_fusion
  66.4 0.0 collective-permute-done.5
  66.4 1.2 add_select_fusion.1
  67.6 1.3 collective-permute-start.6
  69.0 1.3 collective-permute-start.3
  70.3 0.8 dynamic_slice.3
  71.1 2.3 %collective-permute-done.3 = f32[20]{0:T(128)S(1)} collective-permute-done((f32[20]{0:T(128)S(1)}, f32[20]{0:T(128)S(1)}, u32[]{:S(2)}, u32[]{:S(2)}) %collective-permute-start.3) | collective-permute-done | bytes 112 | tf_op jit(solution)/shard_map/ppermute | solution.py:19
  73.3 1.1 fusion.61
  74.5 25.8 %collective-permute-done.6 = f32[20,64,128]{2,1,0:T(8,128)S(1)} collective-permute-done((f32[20,64,128]{2,1,0:T(8,128)S(1)}, f32[20,64,128]{2,1,0:T(8,128)S(1)}, u32[]{:S(2)}, u32[]{:S(2)}) %collective-permute-start.6) | collective-permute-done | bytes 655392 | tf_op jit(solution)/shard_map/ppermute | solution.py:19
  100.3 0.2 fusion.34
  100.5 2.1 %collective-permute-start.7 = (bf16[20,64,128]{2,1,0:T(8,128)(2,1)S(1)}, bf16[20,64,128]{2,1,0:T(8,128)(2,1)S(1)}, u32[]{:S(2)}, u32[]{:S(2)}) collective-permute-start(bf16[20,64,128]{2,1,0:T(8,128)(2,1)S(1)} %fusion.34), channel_id=1, source_target_pairs={{0,4},{4,8},{8,12},{12,16},{16,20},{20,24},{24,28},{1,5},{5,9},{9,... | collective-permute-start | bytes 983048 | tf_op jit(solution)/shard_map/ppermute | solution.py:19
  102.6 1.9 %fusion = f32[4,20,64,128]{3,2,1,0:T(8,128)S(1)} fusion(f32[4,20,128]{2,1,0:T(8,128)S(1)} %copy.17, f32[4,20,128]{2,1,0:T(8,128)S(1)} %reduce_window_sum.11, f32[4,128,128]{2,1,0:T(8,128)S(1)} %fusion.61, pred[128,128]{1,0:T(8,128)(4,1)S(1)} %iota_compare_fusion, bf16[4,128,20,64]{1,0,3,2:T(4,128)(2,1)S(1)} %copy-done), kind=kOutput, calls=%fused_computation.8 | convolution fusion | flops 175636480 | bytes 4292608 | tf_op jit(solution)/shard_map/chts,cshp->cthp/dot_general | solution.py:61
  104.5 6.8 %collective-permute-done.7 = bf16[20,64,128]{2,1,0:T(8,128)(2,1)S(1)} collective-permute-done((bf16[20,64,128]{2,1,0:T(8,128)(2,1)S(1)}, bf16[20,64,128]{2,1,0:T(8,128)(2,1)S(1)}, u32[]{:S(2)}, u32[]{:S(2)}) %collective-permute-start.7) | collective-permute-done | bytes 327712 | tf_op jit(solution)/shard_map/ppermute | solution.py:19
  111.3 0.4 fusion.47
  111.7 0.8 fusion.2
  112.6 1.9 %copy.21 = f32[4,128,20,64]{1,0,3,2:T(4,128)S(1)} copy(f32[4,128,20,64]{1,3,2,0:T(8,128)S(1)} %fusion.2) | data formatting | bytes 5242880 | tf_op jit(solution)/shard_map/add | solution.py:89
  114.6 1.0 fusion.7
  115.6 7.2 %psum.7 = f32[512]{0:T(512)S(1)} all-reduce(f32[512]{0:T(512)S(1)} %get-tuple-element.13), channel_id=1, replica_groups=mesh['seq'=8,'head'=4] {'head'}, use_global_device_ids=true, to_apply=%region_2.3 | all-reduce | flops 512 | bytes 4096 | tf_op jit(solution)/shard_map/psum | solution.py:94
  122.8 7.9 %convolution_convert_fusion = bf16[512,2560]{1,0:T(8,128)(2,1)} fusion(bf16[1280,2560]{1,0:T(8,128)(2,1)} %param.21, bf16[512,1280]{0,1:T(8,128)(2,1)S(1)} %get-tuple-element.14, f32[1280]{0:T(1024)S(1)} %dynamic_slice.3, f32[512]{0:T(512)S(1)} %add_rsqrt_fusion), kind=kOutput, calls=%fused_computation.1 | convolution fusion | flops 3359375360 | bytes 10492928 | tf_op jit(solution)/shard_map/dot_general | solution.py:102
  130.7 34.7 %reduce-scatter.2.cloned.1.call-done = bf16[128,2560]{1,0:T(8,128)(2,1)} async-done(((bf16[512,2560]{1,0:T(8,128)(2,1)}), bf16[128,2560]{1,0:T(8,128)(2,1)}) %reduce-scatter.2.cloned.1.call-update) | async-done | bytes 655376 | tf_op jit(solution)/shard_map/reduce_scatter | solution.py:101
  (48 shorter events, 0.2 us)
Async XLA Ops:
  6.5 14.7 %copy-start.5 = (bf16[512,256]{1,0:T(8,128)(2,1)S(1)}, bf16[512,256]{1,0:T(8,128)(2,1)}, u32[]{:S(2)}) copy-start(bf16[512,256]{1,0:T(8,128)(2,1)} %param.13) | copy-start | bytes 786436
  6.5 158.9 %reduce-scatter.2.cloned.1.call-start = ((), (), s32[]{:S(2)}) async-start(), calls=%async_computation.1 | async-start | bytes 3276800 | tf_op jit(solution)/shard_map/reduce_scatter | solution.py:101
  7.6 14.7 %collective-permute-start = (bf16[3,1280]{0,1:T(8,128)(2,1)S(1)}, bf16[3,1280]{0,1:T(8,128)(2,1)S(1)}, u32[]{:S(2)}, u32[]{:S(2)}) collective-permute-start(bf16[3,1280]{0,1:T(8,128)(2,1)S(1)} %copy.13), channel_id=1, source_target_pairs={{0,4},{4,8},{8,12},{12,16},{16,20},{20,24},{24,28},{1,5},{5,9},{9,... | collective-permute-start | bytes 23048 | tf_op jit(solution)/shard_map/ppermute | solution.py:19
  11.4 9.8 %collective-permute-start.1 = (bf16[3,256]{1,0:T(4,128)(2,1)S(1)}, bf16[3,256]{1,0:T(4,128)(2,1)S(1)}, u32[]{:S(2)}, u32[]{:S(2)}) collective-permute-start(bf16[3,256]{1,0:T(4,128)(2,1)S(1)} %slice.98), channel_id=1, source_target_pairs={{0,4},{4,8},{8,12},{12,16},{16,20},{20,24},{24,28},{1,5},{5,9},{9,... | collective-permute-start | bytes 4616 | tf_op jit(solution)/shard_map/ppermute | solution.py:19
  16.5 5.8 %copy-start.6 = (f32[20]{0:T(128)}, f32[20]{0:T(128)S(1)}, u32[]{:S(2)}) copy-start(f32[20]{0:T(128)S(1)} %get-tuple-element.5) | copy-start | bytes 244
  16.5 5.8 %copy-start.8 = (f32[20]{0:T(128)}, f32[20]{0:T(128)S(1)}, u32[]{:S(2)}) copy-start(f32[20]{0:T(128)S(1)} %get-tuple-element.8) | copy-start | bytes 244
  16.5 5.8 %copy-start.11 = (f32[20]{0:T(128)}, f32[20]{0:T(128)S(1)}, u32[]{:S(2)}) copy-start(f32[20]{0:T(128)S(1)} %get-tuple-element.6) | copy-start | bytes 244
  16.5 5.8 %copy-start.13 = (f32[20]{0:T(128)}, f32[20]{0:T(128)S(1)}, u32[]{:S(2)}) copy-start(f32[20]{0:T(128)S(1)} %get-tuple-element.7) | copy-start | bytes 244
  27.3 1.8 %copy-start.7 = (f32[20]{0:T(128)S(1)}, f32[20]{0:T(128)}, u32[]{:S(2)}) copy-start(f32[20]{0:T(128)} %copy-done.6) | copy-start | bytes 244
  27.3 1.8 %copy-start.10 = (f32[20]{0:T(128)S(1)}, f32[20]{0:T(128)}, u32[]{:S(2)}) copy-start(f32[20]{0:T(128)} %get-tuple-element.31) | copy-start | bytes 244
  27.3 1.8 %copy-start.12 = (f32[20]{0:T(128)S(1)}, f32[20]{0:T(128)}, u32[]{:S(2)}) copy-start(f32[20]{0:T(128)} %copy-done.11) | copy-start | bytes 244
  27.3 1.9 %copy-start.14 = (f32[20]{0:T(128)S(1)}, f32[20]{0:T(128)}, u32[]{:S(2)}) copy-start(f32[20]{0:T(128)} %copy-done.13) | copy-start | bytes 244
  30.3 18.2 %copy-start.2 = (f32[20,64,128]{2,1,0:T(8,128)}, f32[20,64,128]{2,1,0:T(8,128)S(1)}, u32[]{:S(2)}) copy-start(f32[20,64,128]{2,1,0:T(8,128)S(1)} %get-tuple-element.18) | copy-start | bytes 1966084
  30.3 18.2 %collective-permute-start.4 = (f32[20,64,128]{2,1,0:T(8,128)S(1)}, f32[20,64,128]{2,1,0:T(8,128)}, u32[]{:S(2)}, u32[]{:S(2)}) collective-permute-start(f32[20,64,128]{2,1,0:T(8,128)S(1)} %get-tuple-element.18), channel_id=1, source_target_pairs={{0,4},{4,8},{8,12},{12,16},{16,20},{20,24},{24,28},{1,5},{5,9},{9,... | collective-permute-start | bytes 1966088 | tf_op jit(solution)/shard_map/ppermute | solution.py:19
  49.9 16.5 %collective-permute-start.5 = (f32[20,64,128]{2,1,0:T(8,128)S(1)}, f32[20,64,128]{2,1,0:T(8,128)}, u32[]{:S(2)}, u32[]{:S(2)}) collective-permute-start(f32[20,64,128]{2,1,0:T(8,128)S(1)} %add_select_fusion.2), channel_id=1, source_target_pairs={{0,8},{4,12},{8,16},{12,20},{16,24},{20,28},{1,9},{5,13},{9,17},{1... | collective-permute-start | bytes 1966088 | tf_op jit(solution)/shard_map/ppermute | solution.py:19
  51.2 14.5 %collective-permute-start.2 = (f32[20]{0:T(128)}, f32[20]{0:T(128)}, u32[]{:S(2)}, u32[]{:S(2)}) collective-permute-start(f32[20]{0:T(128)} %get-tuple-element.15), channel_id=1, source_target_pairs={{0,4},{4,8},{8,12},{12,16},{16,20},{20,24},{24,28},{1,5},{5,9},{9,... | collective-permute-start | bytes 248 | tf_op jit(solution)/shard_map/ppermute | solution.py:19
  55.6 46.9 %copy-start = (bf16[4,128,20,64]{1,0,3,2:T(4,128)(2,1)S(1)}, bf16[4,128,20,64]{1,0,3,2:T(4,128)(2,1)}, u32[]{:S(2)}) copy-start(bf16[4,128,20,64]{1,0,3,2:T(4,128)(2,1)} %reshape.93) | copy-start | bytes 3932164
  67.6 32.6 %collective-permute-start.6 = (f32[20,64,128]{2,1,0:T(8,128)S(1)}, f32[20,64,128]{2,1,0:T(8,128)S(1)}, u32[]{:S(2)}, u32[]{:S(2)}) collective-permute-start(f32[20,64,128]{2,1,0:T(8,128)S(1)} %add_select_fusion.1), channel_id=1, source_target_pairs={{0,16},{4,20},{8,24},{12,28},{1,17},{5,21},{9,25},{13,29},{2,18},{... | collective-permute-start | bytes 1966088 | tf_op jit(solution)/shard_map/ppermute | solution.py:19
  69.0 4.4 %collective-permute-start.3 = (f32[20]{0:T(128)S(1)}, f32[20]{0:T(128)S(1)}, u32[]{:S(2)}, u32[]{:S(2)}) collective-permute-start(f32[20]{0:T(128)S(1)} %broadcast_select_fusion), channel_id=1, source_target_pairs={{0,8},{4,12},{8,16},{12,20},{16,24},{20,28},{1,9},{5,13},{9,17},{1... | collective-permute-start | bytes 248 | tf_op jit(solution)/shard_map/ppermute | solution.py:19
  100.4 10.9 %copy-start.3 = (f32[20,64,128]{2,1,0:T(8,128)S(1)}, f32[20,64,128]{2,1,0:T(8,128)}, u32[]{:S(2)}) copy-start(f32[20,64,128]{2,1,0:T(8,128)} %get-tuple-element.19) | copy-start | bytes 1966084
  100.5 10.9 %copy-start.9 = (f32[20]{0:T(128)S(1)}, f32[20]{0:T(128)}, u32[]{:S(2)}) copy-start(f32[20]{0:T(128)} %copy-done.8) | copy-start | bytes 244
  100.5 10.9 %copy-start.15 = (f32[20]{0:T(128)S(1)}, f32[20]{0:T(128)}, u32[]{:S(2)}) copy-start(f32[20]{0:T(128)} %get-tuple-element.16) | copy-start | bytes 244
  100.5 10.9 %copy-start.16 = (f32[20]{0:T(128)S(1)}, f32[20]{0:T(128)}, u32[]{:S(2)}) copy-start(f32[20]{0:T(128)} %get-tuple-element.17) | copy-start | bytes 244
  100.5 10.8 %collective-permute-start.7 = (bf16[20,64,128]{2,1,0:T(8,128)(2,1)S(1)}, bf16[20,64,128]{2,1,0:T(8,128)(2,1)S(1)}, u32[]{:S(2)}, u32[]{:S(2)}) collective-permute-start(bf16[20,64,128]{2,1,0:T(8,128)(2,1)S(1)} %fusion.34), channel_id=1, source_target_pairs={{0,4},{4,8},{8,12},{12,16},{16,20},{20,24},{24,28},{1,5},{5,9},{9,... | collective-permute-start | bytes 983048 | tf_op jit(solution)/shard_map/ppermute | solution.py:19
  104.5 7.3 %copy-start.4 = (bf16[512,128]{1,0:T(8,128)(2,1)S(1)}, bf16[512,128]{1,0:T(8,128)(2,1)}, u32[]{:S(2)}) copy-start(bf16[512,128]{1,0:T(8,128)(2,1)} %get-tuple-element.26) | copy-start | bytes 393220
  104.5 7.3 %copy-start.17 = (f32[20]{0:T(128)S(1)}, f32[20]{0:T(128)}, u32[]{:S(2)}) copy-start(f32[20]{0:T(128)} %param.19) | copy-start | bytes 244
  112.6 2.0 %copy-start.1 = (bf16[512,1280]{0,1:T(8,128)(2,1)S(1)}, bf16[512,1280]{0,1:T(8,128)(2,1)}, u32[]{:S(2)}) copy-start(bf16[512,1280]{0,1:T(8,128)(2,1)} %copy.22) | copy-start | bytes 3932164
Sparse Core Ops, SparseCore 0:
  130.9 34.5 reduce-scatter.1
where the time goes:
time: 175 us; the launch traced here: 172 us
  waiting for transfers between devices  96.1 us (55%)
  starting transfers between devices  14.8 us (8%)
  between operations  13.8 us (8%)
  other arithmetic  13.5 us (8%)
  matrix products  13.5 us (8%)
  local copies, waits for them, and re-layouts  13.3 us (8%)
  blocking collectives  7.23 us (4%)
    ppermute x8, waiting for transfers between devices, passed_along(): return lax.ppermute(block, axis, route)  61.3 us
    reduce_scatter x1, waiting for transfers between devices, per_device(): lax.psum_scatter(jnp.dot(normed, w_out, preferred_element_type=jnp.float3...  34.7 us
    ppermute x8, starting transfers between devices, passed_along(): return lax.ppermute(block, axis, route)  14.8 us
    dot_general x1, matrix products, per_device(): jnp.dot(normed, w_out, preferred_element_type=jnp.float32)  7.91 us
    psum x1, blocking collectives, per_device(): sum_squares = lax.psum(partial_sums, 'head')  7.23 us
    unnamed x38, local copies, waits for them, and re-layouts  4.12 us
    convert_element_type x2, other arithmetic, conv_silu(): return jax.nn.silu(summed).astype(jnp.bfloat16)  4.1 us
  transfers between devices with their start and end apart: 9, of which 6 were waited for; matrix products, arithmetic and copies ran while one was open for 10% of the time, Pallas kernels for 0%

commit v1 on v0

v1 whole, which is shorter than its diff:
```python
import functools

import jax
import jax.numpy as jnp
from jax import lax
from jax.experimental import pallas as pl
from jax.experimental.pallas import tpu as pltpu
from jax.sharding import PartitionSpec as P

HEAD_DIM = 64
STATE = 128
CONV = 4
GROUP = 128
LANES = 128
HALO = 16
COLS = 512
EPSILON = 1e-05
MESH = pl.DeviceIdType.MESH
F32 = jnp.float32
BF16 = jnp.bfloat16
HIGH = lax.Precision.HIGHEST


def silu(v):
    half = 0.5 * v
    return half + half * jnp.tanh(half)


def dot(a, b):
    return jnp.dot(a, b, preferred_element_type=F32)


def dot_nt(a, b):
    return lax.dot_general(a, b, (((1,), (1,)), ((), ())), precision=HIGH, preferred_element_type=F32)


def split(v):
    high = v.astype(BF16)
    return high, (v - high.astype(F32)).astype(BF16)


def kernel(
    n_seq, n_head, d_inner,
    x_hbm, z_hbm, bc_hbm, w_hbm, convx, convbc, dt_raw, dt_bias, a_log, skip, gain,
    out,
    xv, zv, bcv, wv, hx, hbc, xf, bcf, xs, cs, bt, dts, las, cum_t, row_t, te_hi, te_lo, ef_hi, ef_lo, emat, skipx,
    exp_f, pre, est, hl, dm, hpart, dpart, prev, psend, csend, inc, aa, bf, gn, acc,
    tosib, fromsib, keep, ysend, yrecv, ssend, srecv,
    load_sem, halo_send, halo_recv, a_send, a_recv, d_send, d_recv, b_send, b_recv, c_send, c_recv,
    sib_send, sib_recv, y_send, y_recv, s_send, s_recv,
):
    rows, width = xv.shape
    heads = dt_raw.shape[0]
    hp = las.shape[0]
    nb, nj = rows // GROUP, width // LANES
    d_model = wv.shape[1]
    own = out.shape[0]
    ncol = d_model // COLS
    n_chip = n_head // 2
    s = lax.axis_index("seq")
    hid = lax.axis_index("head")
    par, pair, npair = lax.rem(s, 2), s // 2, n_seq // 2
    partner = s + 1 - 2 * par
    chip, core = hid // 2, lax.rem(hid, 2)
    sibling = hid + 1 - 2 * core

    loads = [
        pltpu.make_async_copy(bc_hbm, bcv, load_sem.at[0]),
        pltpu.make_async_copy(x_hbm, xv, load_sem.at[1]),
        pltpu.make_async_copy(z_hbm, zv, load_sem.at[2]),
        pltpu.make_async_copy(w_hbm, wv, load_sem.at[3]),
    ]
    for load in loads:
        load.start()

    barrier = pltpu.get_barrier_semaphore()
    count = 0
    for off in (-2, -1, 1, 2):
        there = jnp.logical_and(s + off >= 0, s + off < n_seq)

        @pl.when(there)
        def _():
            pl.semaphore_signal(barrier, inc=1, device_id={"seq": s + off}, device_id_type=MESH)

        count = count + jnp.where(there, 1, 0)
    for d in range(1, n_head):
        pl.semaphore_signal(
            barrier, inc=1, device_id={"head": lax.rem(hid + d, n_head)}, device_id_type=MESH
        )
    pl.semaphore_wait(barrier, count + n_head - 1)

    def remote(src, dst, send, recv, axis, to):
        return pltpu.make_async_remote_copy(
            src_ref=src, dst_ref=dst, send_sem=send, recv_sem=recv,
            device_id={axis: to}, device_id_type=MESH,
        )

    halo_x = remote(x_hbm.at[pl.ds(rows - HALO, HALO)], hx, halo_send.at[0], halo_recv.at[0], "seq", s + 1)
    halo_b = remote(bc_hbm.at[pl.ds(rows - HALO, HALO)], hbc, halo_send.at[1], halo_recv.at[1], "seq", s + 1)

    @pl.when(s < n_seq - 1)
    def _():
        halo_b.start()
        halo_x.start()

    @pl.when(s == 0)
    def _():
        hx[...] = jnp.zeros_like(hx)
        hbc[...] = jnp.zeros_like(hbc)

    @pl.when(pair == 0)
    def _():
        prev[...] = jnp.zeros_like(prev)

    raw = dt_raw[...] + dt_bias[...]
    dt = jnp.maximum(raw, 0.0) + jnp.log(1.0 + jnp.exp(-jnp.abs(raw)))
    dts[...] = jnp.ones_like(dts)
    las[...] = jnp.zeros_like(las)
    dts[0:heads, :] = dt
    las[0:heads, :] = dt * (-jnp.exp(a_log[...]))
    ti = lax.broadcasted_iota(jnp.int32, (GROUP, GROUP), 0)
    si = lax.broadcasted_iota(jnp.int32, (GROUP, GROUP), 1)
    causal = ti >= si
    tri = causal.astype(F32)
    eye = (ti == si).astype(F32)
    emat[...] = (
        lax.broadcasted_iota(jnp.int32, (hp, width), 1) // HEAD_DIM
        == lax.broadcasted_iota(jnp.int32, (hp, width), 0)
    ).astype(F32).astype(BF16)
    for c in range(nb):
        blk = slice(c * GROUP, (c + 1) * GROUP)
        dt_c, la_c = dts[:, blk], las[:, blk]
        cum = dot_nt(tri, la_c)
        cum_t[blk, :] = cum
        row_t[c] = dot_nt(la_c, tri) - jnp.log(dt_c)
        te = jnp.exp(cum[GROUP - 1 :, :] - cum) * dot_nt(eye, dt_c)
        te_hi[blk, :], te_lo[blk, :] = split(te)
        ef_hi[blk, :], ef_lo[blk, :] = split(jnp.exp(cum))
    sk = jnp.where(
        lax.broadcasted_iota(jnp.int32, (heads, width), 1) // HEAD_DIM
        == lax.broadcasted_iota(jnp.int32, (heads, width), 0),
        skip[...], 0.0,
    )
    skipx[...] = jnp.broadcast_to(jnp.sum(sk, axis=0, keepdims=True), skipx.shape)

    loads[0].wait()
    loads[1].wait()

    @pl.when(s > 0)
    def _():
        halo_b.wait_recv()
        halo_x.wait_recv()

    bcf[0:8, :] = hbc[...].astype(F32)[HALO - 8 :]
    bcf[8:, :] = bcv[...].astype(F32)
    conv = convbc[0:1, :] * bcf[pl.ds(9 - CONV, rows), :]
    for k in range(1, CONV):
        conv = conv + convbc[k : k + 1, :] * bcf[pl.ds(9 - CONV + k, rows), :]
    bcs = silu(conv).astype(BF16)
    cs[...] = bcs[:, STATE:]
    for c in range(nb):
        bt[c] = bcs[c * GROUP : (c + 1) * GROUP, :STATE].astype(F32).T.astype(BF16)

    def sends_a(j):
        return (
            remote(hl.at[j], hpart.at[j], a_send.at[j], a_recv.at[j], "seq", partner),
            remote(dm.at[j], dpart.at[j], d_send.at[j], d_recv.at[j], "seq", partner),
        )

    def send_b(j):
        return remote(psend.at[j], prev.at[j], b_send.at[j], b_recv.at[j], "seq", s + 2)

    def send_c(j):
        return remote(csend.at[j], inc.at[j], c_send.at[j], c_recv.at[j], "seq", partner)

    def lanes_of(j):
        return pl.ds(pl.multiple_of(j * LANES, LANES), LANES)

    def own_state(j, carry):
        ln = lanes_of(j)
        xf[0:8, :] = hx[:, ln].astype(F32)[HALO - 8 :]
        xf[8:, :] = xv[:, ln].astype(F32)
        cx = convx[:, ln]
        total = cx[0:1, :] * xf[pl.ds(9 - CONV, rows), :]
        for k in range(1, CONV):
            total = total + cx[k : k + 1, :] * xf[pl.ds(9 - CONV + k, rows), :]
        xb = silu(total).astype(BF16)
        xs[:, ln] = xb
        em = emat[:, ln]
        u = (xb.astype(F32) * (dot(te_hi[...], em) + dot(te_lo[...], em))).astype(BF16)
        ef = dot(ef_hi[...], em) + dot(ef_lo[...], em)
        exp_f[:, ln] = ef
        run = jnp.zeros((STATE, LANES), F32)
        carried = jnp.ones((1, LANES), F32)
        for c in range(nb):
            blk = slice(c * GROUP, (c + 1) * GROUP)
            est[c, :, ln] = run.astype(BF16)
            pre[c, :, ln] = jnp.broadcast_to(carried, (8, LANES))
            decay = ef[(c + 1) * GROUP - 1 : (c + 1) * GROUP, :]
            run = decay * run + dot(bt[c], u[blk])
            carried = carried * decay
        hl[j] = run.astype(BF16)
        dm[j] = jnp.broadcast_to(carried, (8, LANES))

        @pl.when(lax.rem(j, 2) != par)
        def _():
            for copy in sends_a(j):
                copy.start()

        return carry

    lax.fori_loop(0, nj, own_state, 0)
    loads[2].wait()

    lane = lax.broadcasted_iota(jnp.int32, (GROUP, LANES), 1)

    def block(c, carry):
        tk = pl.ds(pl.multiple_of(c * GROUP, GROUP), GROUP)
        c_c = cs[tk, :]
        cb = dot(c_c, bt[c])
        cum = cum_t[tk, :]
        row = row_t[c]
        for j in range(nj):
            ln = slice(j * LANES, (j + 1) * LANES)
            x = xs[tk, ln]
            y = skipx[0:1, ln] * x.astype(F32)
            for k in range(2):
                h = 2 * j + k
                seg = cum[:, h : h + 1] - row[h : h + 1, :]
                g = (cb * jnp.exp(jnp.where(causal, seg, -1e30))).astype(BF16)
                y = y + dot(g, jnp.where((lane < HEAD_DIM) == (k == 0), x, jnp.zeros_like(x)))
            ef = exp_f[tk, ln]
            y = y + ef * dot(c_c, est[c, :, ln])
            sz = silu(zv[tk, ln].astype(F32))
            aa[tk, ln] = y * sz
            bf[tk, ln] = ef * pre[c, 0:1, ln] * sz
        return carry

    early = jnp.minimum(pair, nb)
    lax.fori_loop(0, early, block, 0)

    def serve(i, carry):
        j = 2 * i + par
        for copy in sends_a(j):
            copy.wait_recv()

        @pl.when(pair > 0)
        def _():
            send_b(j).wait_recv()

        first = par == 0
        h_me, h_other = hl[j].astype(F32), hpart[j].astype(F32)
        d_me, d_other = dm[j, 0:1, :], dpart[j, 0:1, :]
        h0, h1 = jnp.where(first, h_me, h_other), jnp.where(first, h_other, h_me)
        d0, d1 = jnp.where(first, d_me, d_other), jnp.where(first, d_other, d_me)
        in0 = prev[j].astype(F32)
        in1 = d0 * in0 + h0

        @pl.when(pair < npair - 1)
        def _():
            psend[j] = (d1 * in1 + h1).astype(BF16)
            send_b(j).start()

        csend[j] = jnp.where(first, in1, in0).astype(BF16)
        send_c(j).start()
        inc[j] = jnp.where(first, in0, in1).astype(BF16)
        return carry

    lax.fori_loop(0, nj // 2, serve, 0)
    lax.fori_loop(early, nb, block, 0)

    acc[...] = jnp.zeros_like(acc)

    def gate(j):
        ln = lanes_of(j)
        g = (aa[:, ln] + bf[:, ln] * dot(cs[...], inc[j])).astype(BF16).astype(F32)
        acc[...] += g * g
        gn[:, ln] = (g * gain[hid, :, ln]).astype(BF16)

    def gate_own(i, carry):
        gate(2 * i + par)
        return carry

    def gate_sent(i, carry):
        j = 2 * i + 1 - par
        send_c(j).wait_recv()
        gate(j)
        return carry

    lax.fori_loop(0, nj // 2, gate_own, 0)
    lax.fori_loop(0, nj // 2, gate_sent, 0)
    loads[3].wait()

    far = (n_chip - 1) * ncol

    def sib(e):
        return remote(tosib.at[e], fromsib.at[e], sib_send.at[e], sib_recv.at[e], "head", sibling)

    def chip_of(e):
        return lax.rem(chip + e // ncol + 1, n_chip)

    def over(e):
        return remote(ysend.at[e], yrecv.at[e], y_send.at[e], y_recv.at[e], "head", chip_of(e) * 2 + core)

    def project(e):
        base = chip_of(e) * 2
        n = lax.rem(e, ncol)
        theirs = gn[pl.ds(pl.multiple_of((base + 1 - core) * own, own), own), :]
        mine = gn[pl.ds(pl.multiple_of((base + core) * own, own), own), :]
        part = dot(
            jnp.concatenate([theirs, mine], axis=0),
            wv[:, pl.ds(pl.multiple_of(n * COLS, COLS), COLS)],
        )
        tosib[e] = part[:own].astype(BF16)
        sib(e).start()
        keep[e] = part[own:]

    def forward(e):
        sib(e).wait_recv()
        ysend[e] = (keep[e] + fromsib[e].astype(F32)).astype(BF16)
        over(e).start()

    def ssq_send(d):
        to = lax.rem(hid + d, n_head)
        return remote(ssend.at[to], srecv.at[d], s_send.at[d], s_recv.at[d], "head", to)

    def step(e, carry):
        project(e)

        @pl.when(jnp.logical_and(e > 0, e <= far))
        def _():
            forward(e - 1)

        return carry

    lax.fori_loop(0, far + ncol, step, 0)

    for b in range(n_head):
        flipped = acc[b * own : (b + 1) * own, :].T
        ssend[b] = jnp.broadcast_to(jnp.sum(flipped, axis=0, keepdims=True), ssend.shape[1:])
    for d in range(1, n_head):
        ssq_send(d).start()
    ssq = ssend[hid]
    for d in range(1, n_head):
        ssq_send(d).wait_recv()
        ssq = ssq + srecv[d]
    inv = lax.rsqrt(ssq[0:1, :] / d_inner + EPSILON)
    inv = jnp.broadcast_to(inv, (LANES, own)).T[:, 0:1]

    def finish(n, carry):
        e = far + n
        sib(e).wait_recv()
        total = keep[e] + fromsib[e].astype(F32)
        for r in range(n_chip - 1):
            over(r * ncol + n).wait_recv()
            total = total + yrecv[r * ncol + n].astype(F32)
        out[:, pl.ds(pl.multiple_of(n * COLS, COLS), COLS)] = (total * inv).astype(BF16)
        return carry

    lax.fori_loop(0, ncol, finish, 0)

    @pl.when(s < n_seq - 1)
    def _():
        halo_b.wait_send()
        halo_x.wait_send()

    def left(i, carry):
        for copy in sends_a(2 * i + 1 - par):
            copy.wait_send()
        send_c(2 * i + par).wait_send()

        @pl.when(pair < npair - 1)
        def _():
            send_b(2 * i + par).wait_send()

        return carry

    lax.fori_loop(0, nj // 2, left, 0)
    for e in range(far + ncol):
        sib(e).wait_send()
    for e in range(far):
        over(e).wait_send()
    for d in range(1, n_head):
        ssq_send(d).wait_send()


def solution(mesh):
    n_seq, n_head = mesh.shape["seq"], mesh.shape["head"]

    def per_device(x_in, z_gate, bc_in, conv_x, conv_bc, dt_raw, dt_bias, a_log, skip_d, norm_weight, w_out):
        rows, width = x_in.shape
        heads = dt_raw.shape[0]
        d_model = w_out.shape[1]
        hp = -(-heads // 32) * 32
        nb, nj, own, ncol = rows // GROUP, width // LANES, rows // n_head, d_model // COLS
        every, far = (n_head // 2) * ncol, (n_head // 2 - 1) * ncol
        assert nj % 2 == 0 and n_seq % 2 == 0 and n_head % 2 == 0 and own == LANES
        hbm, vmem = pl.BlockSpec(memory_space=pl.ANY), pl.BlockSpec(memory_space=pltpu.VMEM)
        dma = pltpu.SemaphoreType.DMA
        scratch = [
            ((rows, width), BF16), ((rows, width), BF16), ((rows, 2 * STATE), BF16), (w_out.shape, BF16),
            ((HALO, width), BF16), ((HALO, 2 * STATE), BF16),
            ((rows + 8, LANES), F32), ((rows + 8, 2 * STATE), F32),
            ((rows, width), BF16), ((rows, STATE), BF16), ((nb, STATE, GROUP), BF16),
            ((hp, rows), F32), ((hp, rows), F32), ((rows, hp), F32), ((nb, hp, GROUP), F32),
            ((rows, hp), BF16), ((rows, hp), BF16), ((rows, hp), BF16), ((rows, hp), BF16),
            ((hp, width), BF16), ((8, width), F32),
            ((rows, width), F32), ((nb, 8, width), F32), ((nb, STATE, width), BF16),
            ((nj, STATE, LANES), BF16), ((nj, 8, LANES), F32), ((nj, STATE, LANES), BF16), ((nj, 8, LANES), F32),
            ((nj, STATE, LANES), BF16), ((nj, STATE, LANES), BF16), ((nj, STATE, LANES), BF16),
            ((nj, STATE, LANES), BF16),
            ((rows, width), F32), ((rows, width), F32), ((rows, width), BF16), ((rows, LANES), F32),
            ((every, own, COLS), BF16), ((every, own, COLS), BF16), ((every, own, COLS), F32),
            ((far, own, COLS), BF16), ((far, own, COLS), BF16),
            ((n_head, 8, own), F32), ((n_head, 8, own), F32),
        ]
        sems = [4, 2, 2] + [nj] * 8 + [every, every, far, far, n_head, n_head]
        return pl.pallas_call(
            functools.partial(kernel, n_seq, n_head, norm_weight.shape[0]),
            out_shape=jax.ShapeDtypeStruct((own, d_model), BF16),
            in_specs=[hbm] * 4 + [vmem] * 7,
            out_specs=vmem,
            scratch_shapes=[pltpu.VMEM(*one) for one in scratch] + [dma((k,)) for k in sems],
            compiler_params=pltpu.CompilerParams(
                collective_id=0, has_side_effects=True, vmem_limit_bytes=60 * 2**20
            ),
        )(
            x_in, z_gate, bc_in, w_out, conv_x, conv_bc, dt_raw, dt_bias[:, None], a_log[:, None],
            skip_d[:, None], norm_weight.reshape(n_head, 1, width),
        )

    in_specs = (
        P("seq", "head"), P("seq", "head"), P("seq", None), P(None, "head"), P(), P("head", "seq"),
        P("head"), P("head"), P("head"), P(), P("head", None),
    )
    return jax.shard_map(
        per_device, mesh=mesh, in_specs=in_specs, out_specs=P(("seq", "head"), None), check_vma=False
    )
```

time: 175 us -> 51.3 us (0.29); the launches traced: 172 us -> 51.1 us
  waiting for transfers between devices: 96.1 us -> 0 us
  Pallas kernels: 0 us -> 45.1 us
  starting transfers between devices: 14.8 us -> 0 us
  between operations: 13.8 us -> 0.01 us
  matrix products: 13.5 us -> 0 us
  other arithmetic: 13.5 us -> 0 us
  local copies, waits for them, and re-layouts: 13.3 us -> 5.97 us
  blocking collectives: 7.23 us -> 0 us
    ppermute x8 -> x0, waiting for transfers between devices: 61.3 us -> none  [passed_along(): return lax.ppermute(block, axis, route)]
    pallas_call x0 -> x1, Pallas kernels: none -> 45.1 us  [per_device(): pl.pallas_call(functools.partial(kernel, n_seq, n_head, norm_weight.shape...]
    reduce_scatter x1 -> x0, waiting for transfers between devices: 34.7 us -> none  [per_device(): lax.psum_scatter(jnp.dot(normed, w_out, preferred_element_type=jnp.float3...]
    ppermute x8 -> x0, starting transfers between devices: 14.8 us -> none  [passed_along(): return lax.ppermute(block, axis, route)]
    dot_general x5 -> x0, matrix products: 13.5 us -> none  [the longest x1 7.91 us: per_device(): jnp.dot(normed, w_out, preferred_element_type=jnp.float32)]
    psum x1 -> x0, blocking collectives: 7.23 us -> none  [per_device(): sum_squares = lax.psum(partial_sums, 'head')]
    slice x7 -> x0, local copies, waits for them, and re-layouts: 4.94 us -> none  [the longest x2 2.37 us: conv_silu(): summed = kernel[0] * extended[0:length].astype(jnp.float32)]
    convert_element_type x3 -> x0, other arithmetic: 4.26 us -> none  [the longest x2 4.1 us: conv_silu(): return jax.nn.silu(summed).astype(jnp.bfloat16)]
  transfers between devices with their start and end apart: 9 -> 0, of which waited for: 6 -> 0; matrix products, arithmetic and copies ran while one was open for 10% -> 0% of each run, Pallas kernels for 0% -> 0%
where the time goes in v1:
time: 51.3 us; the launch traced here: 51.1 us
  Pallas kernels  45.1 us (88%)
  local copies, waits for them, and re-layouts  5.97 us (12%)
    pallas_call x1, Pallas kernels, per_device(): pl.pallas_call(functools.partial(kernel, n_seq, n_head, norm_weight.shape...  45.1 us
    unnamed x1, local copies, waits for them, and re-layouts  1.97 us
    broadcast_in_dim x1, local copies, waits for them, and re-layouts, per_device(): dt_bias[:, None]  1.34 us
    broadcast_in_dim x1, local copies, waits for them, and re-layouts, per_device(): skip_d[:, None]  1.34 us
    broadcast_in_dim x1, local copies, waits for them, and re-layouts, per_device(): a_log[:, None]  1.33 us

profile of v1, /device:TPU:25, one launch (start us, length us, event | category | flops | bytes accessed | tf_op | source)
XLA Modules:
  0.0 51.1 jit_solution(16142322874784147165)
XLA Ops:
  0.0 1.3 %copy.12.dt_bias = f32[20,1]{1,0:T(8,128)} copy(f32[20,1]{0,1:T(1,128)} %bitcast.5) | data formatting | bytes 160 | tf_op jit(solution)/shard_map/broadcast_in_dim | solution.py:428
  1.3 1.3 %copy.13.a_log = f32[20,1]{1,0:T(8,128)} copy(f32[20,1]{0,1:T(1,128)} %bitcast.6) | data formatting | bytes 160 | tf_op jit(solution)/shard_map/broadcast_in_dim | solution.py:428
  2.7 1.3 %copy.14.skip = f32[20,1]{1,0:T(8,128)} copy(f32[20,1]{0,1:T(1,128)} %bitcast.7) | data formatting | bytes 160 | tf_op jit(solution)/shard_map/broadcast_in_dim | solution.py:429
  4.0 45.1 %shard_map.109 = bf16[128,2560]{1,0:T(8,128)(2,1)} custom-call(bf16[512,1280]{1,0:T(8,128)(2,1)} %x_hbm.1, bf16[512,1280]{1,0:T(8,128)(2,1)} %z_hbm.1, bf16[512,256]{1,0:T(8,128)(2,1)} %bc_hbm.1, bf16[1280,2560]{1,0:T(8,128)(2,1)} %w_hbm.1, f32[4,1280]{1,0:T(4,128)} %convx.1, f32[4,256]{1,0:T(4,128)} %convbc.1, f32[20,512]{1,0:T(8,128)} %dt_raw.1, ...), custom_call_target="tpu_custom_call" | custom-call | tf_op jit(solution)/shard_map/pallas_call | solution.py:418
  49.1 2.0 %copy.16 = bf16[128,2560]{1,0:T(8,128)(2,1)} copy(bf16[128,2560]{1,0:T(8,128)(2,1)} %shard_map.109) | data formatting | bytes 1310720

commit v2 on v1

--- a/solution.py
+++ b/solution.py
@@ -13,7 +13,8 @@
 GROUP = 128
 LANES = 128
 HALO = 16
-COLS = 512
+COLS = 256
+LAG = 4
 EPSILON = 1e-05
 MESH = pl.DeviceIdType.MESH
 F32 = jnp.float32
@@ -43,8 +44,8 @@
     n_seq, n_head, d_inner,
     x_hbm, z_hbm, bc_hbm, w_hbm, convx, convbc, dt_raw, dt_bias, a_log, skip, gain,
     out,
-    xv, zv, bcv, wv, hx, hbc, xf, bcf, xs, cs, bt, dts, las, cum_t, row_t, te_hi, te_lo, ef_hi, ef_lo, emat, skipx,
-    exp_f, pre, est, hl, dm, hpart, dpart, prev, psend, csend, inc, aa, bf, gn, acc,
+    xv, zv, bcv, wv, hx, hbc, xf, bcf, xs, cs, bt, dts, las, cum_t, row_t, te_b, end_hi, end_lo, ef_hi, ef_lo, emat, skipx,
+    pre, est, hl, dm, hpart, dpart, prev, psend, csend, inc, aa, bf, gn, acc,
     tosib, fromsib, keep, ysend, yrecv, ssend, srecv,
     load_sem, halo_send, halo_recv, a_send, a_recv, d_send, d_recv, b_send, b_recv, c_send, c_recv,
     sib_send, sib_recv, y_send, y_recv, s_send, s_recv,
@@ -112,12 +113,17 @@
     def _():
         prev[...] = jnp.zeros_like(prev)
 
-    raw = dt_raw[...] + dt_bias[...]
+    same = lax.broadcasted_iota(jnp.int32, (heads, heads), 0) == lax.broadcasted_iota(jnp.int32, (heads, heads), 1)
+
+    def column(row):
+        return jnp.sum(jnp.where(same, row[...], 0.0), axis=1, keepdims=True)
+
+    raw = dt_raw[...] + column(dt_bias)
     dt = jnp.maximum(raw, 0.0) + jnp.log(1.0 + jnp.exp(-jnp.abs(raw)))
     dts[...] = jnp.ones_like(dts)
     las[...] = jnp.zeros_like(las)
     dts[0:heads, :] = dt
-    las[0:heads, :] = dt * (-jnp.exp(a_log[...]))
+    las[0:heads, :] = dt * (-jnp.exp(column(a_log)))
     ti = lax.broadcasted_iota(jnp.int32, (GROUP, GROUP), 0)
     si = lax.broadcasted_iota(jnp.int32, (GROUP, GROUP), 1)
     causal = ti >= si
@@ -134,12 +140,14 @@
         cum_t[blk, :] = cum
         row_t[c] = dot_nt(la_c, tri) - jnp.log(dt_c)
         te = jnp.exp(cum[GROUP - 1 :, :] - cum) * dot_nt(eye, dt_c)
-        te_hi[blk, :], te_lo[blk, :] = split(te)
-        ef_hi[blk, :], ef_lo[blk, :] = split(jnp.exp(cum))
+        te_b[blk, :] = te.astype(BF16)
+        grown = jnp.exp(cum)
+        ef_hi[blk, :], ef_lo[blk, :] = split(grown)
+        end_hi[c], end_lo[c] = split(jnp.broadcast_to(grown[GROUP - 1 :, :], end_hi.shape[1:]))
     sk = jnp.where(
         lax.broadcasted_iota(jnp.int32, (heads, width), 1) // HEAD_DIM
         == lax.broadcasted_iota(jnp.int32, (heads, width), 0),
-        skip[...], 0.0,
+        column(skip), 0.0,
     )
     skipx[...] = jnp.broadcast_to(jnp.sum(sk, axis=0, keepdims=True), skipx.shape)
 
@@ -175,6 +183,33 @@
 
     def lanes_of(j):
         return pl.ds(pl.multiple_of(j * LANES, LANES), LANES)
+
+    def serve(i, carry):
+        j = 2 * i + par
+        for copy in sends_a(j):
+            copy.wait_recv()
+
+        @pl.when(pair > 0)
+        def _():
+            send_b(j).wait_recv()
+
+        first = par == 0
+        h_me, h_other = hl[j].astype(F32), hpart[j].astype(F32)
+        d_me, d_other = dm[j, 0:1, :], dpart[j, 0:1, :]
+        h0, h1 = jnp.where(first, h_me, h_other), jnp.where(first, h_other, h_me)
+        d0, d1 = jnp.where(first, d_me, d_other), jnp.where(first, d_other, d_me)
+        in0 = prev[j].astype(F32)
+        in1 = d0 * in0 + h0
+
+        @pl.when(pair < npair - 1)
+        def _():
+            psend[j] = (d1 * in1 + h1).astype(BF16)
+            send_b(j).start()
+
+        csend[j] = jnp.where(first, in1, in0).astype(BF16)
+        send_c(j).start()
+        inc[j] = jnp.where(first, in0, in1).astype(BF16)
+        return carry
 
     def own_state(j, carry):
         ln = lanes_of(j)
@@ -187,16 +222,14 @@
         xb = silu(total).astype(BF16)
         xs[:, ln] = xb
         em = emat[:, ln]
-        u = (xb.astype(F32) * (dot(te_hi[...], em) + dot(te_lo[...], em))).astype(BF16)
-        ef = dot(ef_hi[...], em) + dot(ef_lo[...], em)
-        exp_f[:, ln] = ef
+        u = (xb.astype(F32) * dot(te_b[...], em)).astype(BF16)
         run = jnp.zeros((STATE, LANES), F32)
         carried = jnp.ones((1, LANES), F32)
         for c in range(nb):
             blk = slice(c * GROUP, (c + 1) * GROUP)
             est[c, :, ln] = run.astype(BF16)
             pre[c, :, ln] = jnp.broadcast_to(carried, (8, LANES))
-            decay = ef[(c + 1) * GROUP - 1 : (c + 1) * GROUP, :]
+            decay = (dot(end_hi[c], em) + dot(end_lo[c], em))[0:1, :]
             run = decay * run + dot(bt[c], u[blk])
             carried = carried * decay
         hl[j] = run.astype(BF16)
@@ -207,9 +240,16 @@
             for copy in sends_a(j):
                 copy.start()
 
+        late = j - LAG
+
+        @pl.when(jnp.logical_and(pair == 0, jnp.logical_and(late >= 0, lax.rem(late + par + 2, 2) == 0)))
+        def _():
+            serve(late // 2, 0)
+
         return carry
 
     lax.fori_loop(0, nj, own_state, 0)
+    done = jnp.where(pair == 0, (nj - LAG + 1 - par) // 2, 0)
     loads[2].wait()
 
     lane = lax.broadcasted_iota(jnp.int32, (GROUP, LANES), 1)
@@ -229,62 +269,45 @@
                 seg = cum[:, h : h + 1] - row[h : h + 1, :]
                 g = (cb * jnp.exp(jnp.where(causal, seg, -1e30))).astype(BF16)
                 y = y + dot(g, jnp.where((lane < HEAD_DIM) == (k == 0), x, jnp.zeros_like(x)))
-            ef = exp_f[tk, ln]
+            em = emat[:, ln]
+            ef = dot(ef_hi[tk, :], em) + dot(ef_lo[tk, :], em)
             y = y + ef * dot(c_c, est[c, :, ln])
             sz = silu(zv[tk, ln].astype(F32))
             aa[tk, ln] = y * sz
             bf[tk, ln] = ef * pre[c, 0:1, ln] * sz
         return carry
 
-    early = jnp.minimum(pair, nb)
+    early = jnp.minimum(jnp.where(pair == npair - 1, pair, jnp.maximum(pair - 1, 0)), nb - 1)
     lax.fori_loop(0, early, block, 0)
 
-    def serve(i, carry):
-        j = 2 * i + par
-        for copy in sends_a(j):
-            copy.wait_recv()
-
-        @pl.when(pair > 0)
-        def _():
-            send_b(j).wait_recv()
-
-        first = par == 0
-        h_me, h_other = hl[j].astype(F32), hpart[j].astype(F32)
-        d_me, d_other = dm[j, 0:1, :], dpart[j, 0:1, :]
-        h0, h1 = jnp.where(first, h_me, h_other), jnp.where(first, h_other, h_me)
-        d0, d1 = jnp.where(first, d_me, d_other), jnp.where(first, d_other, d_me)
-        in0 = prev[j].astype(F32)
-        in1 = d0 * in0 + h0
-
-        @pl.when(pair < npair - 1)
-        def _():
-            psend[j] = (d1 * in1 + h1).astype(BF16)
-            send_b(j).start()
-
-        csend[j] = jnp.where(first, in1, in0).astype(BF16)
-        send_c(j).start()
-        inc[j] = jnp.where(first, in0, in1).astype(BF16)
-        return carry
-
-    lax.fori_loop(0, nj // 2, serve, 0)
+    lax.fori_loop(done, nj // 2, serve, 0)
     lax.fori_loop(early, nb, block, 0)
 
     acc[...] = jnp.zeros_like(acc)
 
-    def gate(j):
+    chip_rows = 2 * own
+
+    def gate(j, r):
         ln = lanes_of(j)
-        g = (aa[:, ln] + bf[:, ln] * dot(cs[...], inc[j])).astype(BF16).astype(F32)
-        acc[...] += g * g
-        gn[:, ln] = (g * gain[hid, :, ln]).astype(BF16)
+        tk = pl.ds(pl.multiple_of(lax.rem(chip + r, n_chip) * chip_rows, chip_rows), chip_rows)
+        g = (aa[tk, ln] + bf[tk, ln] * dot(cs[tk, :], inc[j])).astype(BF16).astype(F32)
+        acc[tk, :] += g * g
+        gn[tk, ln] = (g * gain[hid, :, ln]).astype(BF16)
 
     def gate_own(i, carry):
-        gate(2 * i + par)
+        for r in range(n_chip):
+            gate(2 * i + par, r)
         return carry
 
     def gate_sent(i, carry):
         j = 2 * i + 1 - par
         send_c(j).wait_recv()
-        gate(j)
+        for r in range(1, n_chip):
+            gate(j, r)
+        return carry
+
+    def gate_near(i, carry):
+        gate(2 * i + 1 - par, 0)
         return carry
 
     lax.fori_loop(0, nj // 2, gate_own, 0)
@@ -327,13 +350,20 @@
     def step(e, carry):
         project(e)
 
-        @pl.when(jnp.logical_and(e > 0, e <= far))
+        @pl.when(e > 0)
         def _():
             forward(e - 1)
 
         return carry
 
-    lax.fori_loop(0, far + ncol, step, 0)
+    def near(e, carry):
+        project(e)
+        return carry
+
+    lax.fori_loop(0, far, step, 0)
+    forward(far - 1)
+    lax.fori_loop(0, nj // 2, gate_near, 0)
+    lax.fori_loop(far, far + ncol, near, 0)
 
     for b in range(n_head):
         flipped = acc[b * own : (b + 1) * own, :].T
@@ -403,9 +433,9 @@
             ((rows + 8, LANES), F32), ((rows + 8, 2 * STATE), F32),
             ((rows, width), BF16), ((rows, STATE), BF16), ((nb, STATE, GROUP), BF16),
             ((hp, rows), F32), ((hp, rows), F32), ((rows, hp), F32), ((nb, hp, GROUP), F32),
-            ((rows, hp), BF16), ((rows, hp), BF16), ((rows, hp), BF16), ((rows, hp), BF16),
+            ((rows, hp), BF16), ((nb, 16, hp), BF16), ((nb, 16, hp), BF16), ((rows, hp), BF16), ((rows, hp), BF16),
             ((hp, width), BF16), ((8, width), F32),
-            ((rows, width), F32), ((nb, 8, width), F32), ((nb, STATE, width), BF16),
+            ((nb, 8, width), F32), ((nb, STATE, width), BF16),
             ((nj, STATE, LANES), BF16), ((nj, 8, LANES), F32), ((nj, STATE, LANES), BF16), ((nj, 8, LANES), F32),
             ((nj, STATE, LANES), BF16), ((nj, STATE, LANES), BF16), ((nj, STATE, LANES), BF16),
             ((nj, STATE, LANES), BF16),
@@ -425,8 +455,8 @@
                 collective_id=0, has_side_effects=True, vmem_limit_bytes=60 * 2**20
             ),
         )(
-            x_in, z_gate, bc_in, w_out, conv_x, conv_bc, dt_raw, dt_bias[:, None], a_log[:, None],
-            skip_d[:, None], norm_weight.reshape(n_head, 1, width),
+            x_in, z_gate, bc_in, w_out, conv_x, conv_bc, dt_raw, dt_bias[None], a_log[None],
+            skip_d[None], norm_weight.reshape(n_head, 1, width),
         )
 
     in_specs = (

time: 51.3 us -> 49.6 us (0.967)
  local copies, waits for them, and re-layouts: 5.97 us -> 1.97 us
  Pallas kernels: 45.1 us -> 47.4 us
    broadcast_in_dim x3 -> x0, local copies, waits for them, and re-layouts: 4.01 us -> none  [the longest x1 1.34 us: per_device(): dt_bias[:, None]]
    pallas_call x1, Pallas kernels: 45.1 us -> 47.4 us  [per_device(): pl.pallas_call(functools.partial(kernel, n_seq, n_head, norm_weight.shape...]
where the time goes in v2:
time: 49.6 us; the launch traced here: 49.4 us
  Pallas kernels  47.4 us (96%)
  local copies, waits for them, and re-layouts  1.97 us (4%)
    pallas_call x1, Pallas kernels, per_device(): pl.pallas_call(functools.partial(kernel, n_seq, n_head, norm_weight.shape...  47.4 us
    unnamed x1, local copies, waits for them, and re-layouts  1.97 us

profile of v2, /device:TPU:25, one launch (start us, length us, event | category | flops | bytes accessed | tf_op | source)
XLA Modules:
  0.0 49.4 jit_solution(2591955011446952572)
XLA Ops:
  0.0 47.4 %shard_map.109 = bf16[128,2560]{1,0:T(8,128)(2,1)} custom-call(bf16[512,1280]{1,0:T(8,128)(2,1)} %x_hbm.1, bf16[512,1280]{1,0:T(8,128)(2,1)} %z_hbm.1, bf16[512,256]{1,0:T(8,128)(2,1)} %bc_hbm.1, bf16[1280,2560]{1,0:T(8,128)(2,1)} %w_hbm.1, f32[4,1280]{1,0:T(4,128)} %convx.1, f32[4,256]{1,0:T(4,128)} %convbc.1, f32[20,512]{1,0:T(8,128)} %dt_raw.1, ...), custom_call_target="tpu_custom_call" | custom-call | tf_op jit(solution)/shard_map/pallas_call | solution.py:448
  47.4 2.0 %copy.13 = bf16[128,2560]{1,0:T(8,128)(2,1)} copy(bf16[128,2560]{1,0:T(8,128)(2,1)} %shard_map.109) | data formatting | bytes 1310720

commit v3 on v2

--- a/solution.py
+++ b/solution.py
@@ -13,7 +13,7 @@
 GROUP = 128
 LANES = 128
 HALO = 16
-COLS = 256
+COLS = 512
 LAG = 4
 EPSILON = 1e-05
 MESH = pl.DeviceIdType.MESH
@@ -44,7 +44,7 @@
     n_seq, n_head, d_inner,
     x_hbm, z_hbm, bc_hbm, w_hbm, convx, convbc, dt_raw, dt_bias, a_log, skip, gain,
     out,
-    xv, zv, bcv, wv, hx, hbc, xf, bcf, xs, cs, bt, dts, las, cum_t, row_t, te_b, end_hi, end_lo, ef_hi, ef_lo, emat, skipx,
+    xv, zv, bcv, wv, tx, tbc, hx, hbc, xf, bcf, xs, cs, bt, dts, las, cum_t, row_t, te_b, end_hi, end_lo, ef_hi, ef_lo, emat, skipx,
     pre, est, hl, dm, hpart, dpart, prev, psend, csend, inc, aa, bf, gn, acc,
     tosib, fromsib, keep, ysend, yrecv, ssend, srecv,
     load_sem, halo_send, halo_recv, a_send, a_recv, d_send, d_recv, b_send, b_recv, c_send, c_recv,
@@ -65,13 +65,17 @@
     chip, core = hid // 2, lax.rem(hid, 2)
     sibling = hid + 1 - 2 * core
 
+    tails = [
+        pltpu.make_async_copy(bc_hbm.at[pl.ds(rows - HALO, HALO)], tbc, load_sem.at[4]),
+        pltpu.make_async_copy(x_hbm.at[pl.ds(rows - HALO, HALO)], tx, load_sem.at[5]),
+    ]
     loads = [
         pltpu.make_async_copy(bc_hbm, bcv, load_sem.at[0]),
         pltpu.make_async_copy(x_hbm, xv, load_sem.at[1]),
         pltpu.make_async_copy(z_hbm, zv, load_sem.at[2]),
         pltpu.make_async_copy(w_hbm, wv, load_sem.at[3]),
     ]
-    for load in loads:
+    for load in tails + loads:
         load.start()
 
     barrier = pltpu.get_barrier_semaphore()
@@ -88,6 +92,8 @@
         pl.semaphore_signal(
             barrier, inc=1, device_id={"head": lax.rem(hid + d, n_head)}, device_id_type=MESH
         )
+    for tail in tails:
+        tail.wait()
     pl.semaphore_wait(barrier, count + n_head - 1)
 
     def remote(src, dst, send, recv, axis, to):
@@ -96,8 +102,8 @@
             device_id={axis: to}, device_id_type=MESH,
         )
 
-    halo_x = remote(x_hbm.at[pl.ds(rows - HALO, HALO)], hx, halo_send.at[0], halo_recv.at[0], "seq", s + 1)
-    halo_b = remote(bc_hbm.at[pl.ds(rows - HALO, HALO)], hbc, halo_send.at[1], halo_recv.at[1], "seq", s + 1)
+    halo_x = remote(tx, hx, halo_send.at[0], halo_recv.at[0], "seq", s + 1)
+    halo_b = remote(tbc, hbc, halo_send.at[1], halo_recv.at[1], "seq", s + 1)
 
     @pl.when(s < n_seq - 1)
     def _():
@@ -347,6 +353,21 @@
         to = lax.rem(hid + d, n_head)
         return remote(ssend.at[to], srecv.at[d], s_send.at[d], s_recv.at[d], "head", to)
 
+    def ssq_of(r):
+        to_chip = lax.rem(chip + r, n_chip)
+        for k in range(2):
+            b = to_chip * 2 + k
+            flipped = acc[pl.ds(pl.multiple_of(b * own, own), own), :].T
+            ssend[b] = jnp.broadcast_to(jnp.sum(flipped, axis=0, keepdims=True), ssend.shape[1:])
+        for d in range(1, n_head):
+
+            @pl.when(lax.rem(hid + d, n_head) // 2 == to_chip)
+            def _():
+                ssq_send(d).start()
+
+    for r in range(1, n_chip):
+        ssq_of(r)
+
     def step(e, carry):
         project(e)
 
@@ -363,13 +384,9 @@
     lax.fori_loop(0, far, step, 0)
     forward(far - 1)
     lax.fori_loop(0, nj // 2, gate_near, 0)
+    ssq_of(0)
     lax.fori_loop(far, far + ncol, near, 0)
 
-    for b in range(n_head):
-        flipped = acc[b * own : (b + 1) * own, :].T
-        ssend[b] = jnp.broadcast_to(jnp.sum(flipped, axis=0, keepdims=True), ssend.shape[1:])
-    for d in range(1, n_head):
-        ssq_send(d).start()
     ssq = ssend[hid]
     for d in range(1, n_head):
         ssq_send(d).wait_recv()
@@ -429,7 +446,7 @@
         dma = pltpu.SemaphoreType.DMA
         scratch = [
             ((rows, width), BF16), ((rows, width), BF16), ((rows, 2 * STATE), BF16), (w_out.shape, BF16),
-            ((HALO, width), BF16), ((HALO, 2 * STATE), BF16),
+            ((HALO, width), BF16), ((HALO, 2 * STATE), BF16), ((HALO, width), BF16), ((HALO, 2 * STATE), BF16),
             ((rows + 8, LANES), F32), ((rows + 8, 2 * STATE), F32),
             ((rows, width), BF16), ((rows, STATE), BF16), ((nb, STATE, GROUP), BF16),
             ((hp, rows), F32), ((hp, rows), F32), ((rows, hp), F32), ((nb, hp, GROUP), F32),
@@ -444,7 +461,7 @@
             ((far, own, COLS), BF16), ((far, own, COLS), BF16),
             ((n_head, 8, own), F32), ((n_head, 8, own), F32),
         ]
-        sems = [4, 2, 2] + [nj] * 8 + [every, every, far, far, n_head, n_head]
+        sems = [6, 2, 2] + [nj] * 8 + [every, every, far, far, n_head, n_head]
         return pl.pallas_call(
             functools.partial(kernel, n_seq, n_head, norm_weight.shape[0]),
             out_shape=jax.ShapeDtypeStruct((own, d_model), BF16),

time: 49.6 us -> 48.3 us (0.974)
  Pallas kernels: 47.4 us -> 46.1 us
    pallas_call x1, Pallas kernels: 47.4 us -> 46.1 us  [per_device(): pl.pallas_call(functools.partial(kernel, n_seq, n_head, norm_weight.shape...]
where the time goes in v3:
time: 48.3 us; the launch traced here: 48 us
  Pallas kernels  46.1 us (95%)
  local copies, waits for them, and re-layouts  1.97 us (4%)
    pallas_call x1, Pallas kernels, per_device(): pl.pallas_call(functools.partial(kernel, n_seq, n_head, norm_weight.shape...  46.1 us
    unnamed x1, local copies, waits for them, and re-layouts  1.97 us

profile of v3, /device:TPU:25, one launch (start us, length us, event | category | flops | bytes accessed | tf_op | source)
XLA Modules:
  0.0 48.0 jit_solution(1191379219649599373)
XLA Ops:
  0.0 46.1 %shard_map.109 = bf16[128,2560]{1,0:T(8,128)(2,1)} custom-call(bf16[512,1280]{1,0:T(8,128)(2,1)} %x_hbm.1, bf16[512,1280]{1,0:T(8,128)(2,1)} %z_hbm.1, bf16[512,256]{1,0:T(8,128)(2,1)} %bc_hbm.1, bf16[1280,2560]{1,0:T(8,128)(2,1)} %w_hbm.1, f32[4,1280]{1,0:T(4,128)} %convx.1, f32[4,256]{1,0:T(4,128)} %convbc.1, f32[20,512]{1,0:T(8,128)} %dt_raw.1, ...), custom_call_target="tpu_custom_call" | custom-call | tf_op jit(solution)/shard_map/pallas_call | solution.py:465
  46.1 2.0 %copy.13 = bf16[128,2560]{1,0:T(8,128)(2,1)} copy(bf16[128,2560]{1,0:T(8,128)(2,1)} %shard_map.109) | data formatting | bytes 1310720
